TPU v7x, 32 devices: a whole 2x2x4 slice. The times are simulated.
32 devices in a mesh: rep: 2 (over x), blk: 16 (over z, y, core).
Axes of the slice: x: 2, y: 2, z: 4, core: 2. Of those that a mesh axis runs over, the one named last changes fastest.
Arguments:
- hidden: bfloat16 [32, 4096], P('rep', 'blk'), parts along dimension 0, may hold values from -4 to 4
- queries: bfloat16 [32, 4096], P('rep'), parts along dimension 0, may hold values from -180 to 180
- cache_kv: bfloat16 [2, 32, 512, 1024], P(None, 'rep', 'blk'), parts along dimension 1, may hold values from -6 to 6
- cache_len: int32 [32], P('rep'), parts along dimension 0, may hold values from 1 to 512
- inserted_key_value: bfloat16 [2, 16, 512, 1024], P(None, 'rep', 'blk'), parts along dimension 1, may hold values from -6 to 6
- insert_slot: int32 [16], P('rep'), parts along dimension 0, may hold values from 0 to 15, as said below
- prefix_len: int32 [16], P('rep'), parts along dimension 0, may hold values from 1 to 512, as said below
- out_weight: bfloat16 [4096, 4096], P(None, 'blk'), may hold values from -0.09375 to 0.09375
- norm_gain: bfloat16 [4096], replicated, may hold values from 0.25 to 1.75
- router_weight: bfloat16 [4096, 4], replicated, may hold values from -0.09375 to 0.09375
- expert_ids: int32 [32, 2], P('rep'), parts along dimension 0, may hold values from 0 to 3, all different within a row
- gate_up: bfloat16 [2, 4096, 28672], P(None, None, 'blk'), may hold values from -0.09375 to 0.09375
- down_proj: bfloat16 [28672, 4096], P('blk'), may hold values from -0.0625 to 0.0625
Outputs:
- layer_out: bfloat16 [32, 4096], P('rep', 'blk'), parts along dimension 0
There are 2 independent parts, one for each index of `rep`. A program takes and returns all parts, laid end to end along the dimension named above; an argument that names none is the same for every part. Nothing has to cross between parts.
Inputs may be any that keep to these rules, and one draw needn't show every extreme that they name: `insert_slot`: 8 different slot numbers. `prefix_len`: some inserted request has all 512 positions.
All inputs are finite; a program needn't handle non-finite values.
Results may differ from a plain program's by a relative error of at most 0.012.
Values may be sent and summed in bfloat16 or wider, within the bound.
A program may use at most 128 MiB of HBM per device.

v0:
```python
import math

import jax
import jax.numpy as jnp
from jax import lax
from jax.sharding import PartitionSpec as P

QUERY_HEADS = 32
KEY_VALUE_HEADS = 8
HEAD_SIZE = 128
EXPERTS = 4
FF = 7168


def shifted(shard, axis, by):
    count = lax.axis_size(axis)
    return lax.ppermute(shard, axis, [(i, (i + by) % count) for i in range(count)])


def merged(value, axis, join):
    pieces = jax.tree.map(lambda part: lax.all_gather(part, axis), value)
    head = jax.tree.map(lambda part: part[0], pieces)
    tail = jax.tree.map(lambda part: part[1:], pieces)
    total, _ = lax.scan(lambda total, piece: (join(total, piece), None), head, tail)
    return total


def block_attention(queries, key_rows, value_rows, valid):
    slot_list = queries.shape[0]
    query_groups = QUERY_HEADS // KEY_VALUE_HEADS
    heads_of_queries = queries.astype(jnp.float32).reshape(
        slot_list, KEY_VALUE_HEADS, query_groups, HEAD_SIZE
    )
    heads_of_keys = key_rows.astype(jnp.float32).reshape(slot_list, -1, KEY_VALUE_HEADS, HEAD_SIZE)
    heads_of_values = value_rows.astype(jnp.float32).reshape(
        slot_list, -1, KEY_VALUE_HEADS, HEAD_SIZE
    )
    scores = jnp.einsum("skgd,sckd->skgc", heads_of_queries, heads_of_keys) / math.sqrt(HEAD_SIZE)
    masked = valid[:, None, None, :]
    peak = jnp.max(jnp.where(masked, scores, -1e30), axis=-1)
    weights = jnp.where(masked, jnp.exp(scores - peak[..., None]), 0.0)
    totals = jnp.sum(weights, axis=-1)
    partial_value = jnp.einsum("skgc,sckd->skgd", weights, heads_of_values)
    return (
        partial_value.reshape(slot_list, QUERY_HEADS, HEAD_SIZE),
        peak.reshape(slot_list, QUERY_HEADS),
        totals.reshape(slot_list, QUERY_HEADS),
    )


def merge_pair(earlier, later):
    early_out, early_peak, early_total = earlier
    late_out, late_peak, late_total = later
    highest = jnp.maximum(early_peak, late_peak)
    early_scale = jnp.exp(early_peak - highest)
    late_scale = jnp.exp(late_peak - highest)
    merged_out = early_out * early_scale[..., None] + late_out * late_scale[..., None]
    return (merged_out, highest, early_total * early_scale + late_total * late_scale)


def route_shares(normed, router_weight, expert_ids):
    logits = jnp.dot(normed, router_weight, preferred_element_type=jnp.float32)
    chosen = (expert_ids[:, :, None] == jnp.arange(EXPERTS, dtype=jnp.int32)[None, None, :]).astype(
        jnp.float32
    )
    picked = jnp.sum(chosen * logits[:, None, :], axis=-1)
    gates = jax.nn.sigmoid(picked - picked[:, ::-1])
    return jnp.sum(gates[:, :, None] * chosen, axis=1)


def on_device(
    hidden,
    queries,
    cache_kv,
    cache_len,
    inserted_key_value,
    insert_slot,
    prefix_len,
    out_weight,
    norm_gain,
    router_weight,
    expert_ids,
    gate_up,
    down_proj,
):
    cycle_size = lax.axis_size("blk")
    dev_index = lax.axis_index("blk")
    half_cycle = cycle_size // 2
    ctx_rows = cache_kv.shape[2]
    column_half = inserted_key_value.shape[3] // 2
    first_cols = shifted(inserted_key_value[..., :column_half], "blk", half_cycle)
    second_cols = shifted(inserted_key_value[..., column_half:], "blk", -half_cycle)
    arrived = jnp.concatenate([first_cols, second_cols], axis=3)
    cache = cache_kv.at[:, insert_slot].set(arrived)
    slot_lengths = cache_len.at[insert_slot].set(prefix_len)
    positions = dev_index * ctx_rows + jnp.arange(ctx_rows, dtype=jnp.int32)
    valid = positions[None, :] < slot_lengths[:, None]
    partial_value, peak, totals = block_attention(queries, cache[0], cache[1], valid)
    slot_list = queries.shape[0]
    summed, highest, all_totals = merged((partial_value, peak, totals), "blk", merge_pair)
    attn = (
        (summed / all_totals[..., None])
        .reshape(slot_list, QUERY_HEADS * HEAD_SIZE)
        .astype(jnp.bfloat16)
    )
    local_mixed = (
        hidden.astype(jnp.float32) + jnp.dot(attn, out_weight, preferred_element_type=jnp.float32)
    ).astype(jnp.bfloat16)
    mixed = lax.all_gather(local_mixed, "blk", axis=1, tiled=True)
    mixed_f = mixed.astype(jnp.float32)
    scale = lax.rsqrt(jnp.mean(mixed_f * mixed_f, axis=-1, keepdims=True) + 1e-05)
    normed = (mixed_f * scale * norm_gain.astype(jnp.float32)).astype(jnp.bfloat16)
    shares = route_shares(normed, router_weight, expert_ids)
    unit_count = gate_up.shape[2]
    expert_now = dev_index * unit_count // FF
    picker = (jnp.arange(EXPERTS, dtype=jnp.int32) == expert_now).astype(jnp.float32)
    expert_share = jnp.sum(shares * picker[None, :], axis=1)
    act = (
        jax.nn.silu(jnp.dot(normed, gate_up[0], preferred_element_type=jnp.float32))
        * jnp.dot(normed, gate_up[1], preferred_element_type=jnp.float32)
    ).astype(jnp.bfloat16)
    term = expert_share[:, None] * jnp.dot(act, down_proj, preferred_element_type=jnp.float32)
    moe = lax.psum_scatter(term, "blk", scatter_dimension=1, tiled=True)
    return (local_mixed.astype(jnp.float32) + moe).astype(jnp.bfloat16)


def solution(mesh):
    in_specs = (
        P("rep", "blk"),
        P("rep", None),
        P(None, "rep", "blk", None),
        P("rep"),
        P(None, "rep", "blk", None),
        P("rep"),
        P("rep"),
        P(None, "blk"),
        P(),
        P(),
        P("rep", None),
        P(None, None, "blk"),
        P("blk", None),
    )
    out_specs = P("rep", "blk")
    return jax.shard_map(
        on_device, mesh=mesh, in_specs=in_specs, out_specs=out_specs, check_vma=False
    )
```

profile of v0, /device:TPU:0, one launch (start us, length us, event | category | flops | bytes accessed | tf_op | source)
XLA Modules:
  0.0 245.7 jit_solution(6826515580782197177)
XLA Ops:
  6.5 0.0 copy-start
  6.5 0.0 copy-start.8
  6.6 0.0 all-gather.2.cloned.1.call-start
  6.6 3.4 %copy.72 = bf16[2,16,32,1024]{3,2,1,0:T(8,128)(2,1)} copy(bf16[2,16,32,1024]{3,2,1,0:T(8,128)(2,1)} %param.17) | data formatting | bytes 4194304
  10.0 0.0 copy-done.3
  10.0 1.1 fusion.45
  11.1 4.1 %collective-permute-start.1 = (bf16[2,8,32,512]{3,2,1,0:T(8,128)(2,1)}, bf16[2,8,32,512]{3,2,1,0:T(8,128)(2,1)S(1)}, u32[]{:S(2)}, u32[]{:S(2)}) collective-permute-start(bf16[2,8,32,512]{3,2,1,0:T(8,128)(2,1)} %get-tuple-element.73), channel_id=1, source_target_pairs={{0,8},{1,9},{2,10},{3,11},{4,12},{5,13},{6,14},{7,15},{8,0},{9,1},... | collective-permute-start | bytes 1572872 | tf_op jit(solution)/shard_map/ppermute | solution.py:17
  15.1 0.0 collective-permute-start
  15.2 0.0 copy-done.4
  15.2 0.1 reshape.63
  15.3 0.0 copy-done.10
  15.3 0.0 copy-done.2
  15.3 0.6 scatter_fusion
  15.9 0.1 broadcast_compare_fusion
  16.0 34.6 %collective-permute-done.1 = bf16[2,8,32,512]{3,2,1,0:T(8,128)(2,1)S(1)} collective-permute-done((bf16[2,8,32,512]{3,2,1,0:T(8,128)(2,1)}, bf16[2,8,32,512]{3,2,1,0:T(8,128)(2,1)S(1)}, u32[]{:S(2)}, u32[]{:S(2)}) %collective-permute-start.1) | collective-permute-done | bytes 524320 | tf_op jit(solution)/shard_map/ppermute | solution.py:17
  50.6 10.4 %collective-permute-done = bf16[2,8,32,512]{3,2,1,0:T(8,128)(2,1)S(1)} collective-permute-done((bf16[2,8,32,512]{3,2,1,0:T(8,128)(2,1)}, bf16[2,8,32,512]{3,2,1,0:T(8,128)(2,1)S(1)}, u32[]{:S(2)}, u32[]{:S(2)}) %collective-permute-start) | collective-permute-done | bytes 524320 | tf_op jit(solution)/shard_map/ppermute | solution.py:17
  61.0 0.1 maximum_bitcast_fusion
  61.1 0.1 copy.36
  61.2 2.9 %scatter_fusion.1 = bf16[2,16,32,1024]{3,2,1,0:T(8,128)(2,1)} fusion(bf16[2,16,32,1024]{3,2,1,0:T(8,128)(2,1)} %copy.72, s32[8]{0:T(128)S(1)} %compare_select_fusion, bf16[8,2,32,1024]{3,2,1,0:T(8,128)(2,1)S(1)} %copy.36), kind=kCustom, calls=%fused_computation.1 | custom fusion | bytes 3145760 | tf_op jit(solution)/shard_map/scatter | solution.py:94
  64.1 1.7 fusion.44
  65.8 0.0 copy-start.6
  65.8 0.3 copy.44
  66.1 0.3 copy.43
  66.4 0.7 select_reduce_fusion
  67.1 1.2 fusion.18
  68.3 0.0 all-gather.2.cloned.1.call-update
  68.3 0.0 reduce-scatter.2.cloned.1.call-start
  68.4 0.1 copy.39
  68.5 0.1 copy.40
  68.6 0.4 fusion.24
  69.0 0.1 copy.41
  69.1 0.1 copy.42
  69.2 22.1 %all_gather.13 = f32[16,16,32]{2,1,0:T(8,128)S(1)} all-gather(f32[1,16,32]{2,1,0:T(8,128)S(1)} %copy.40), channel_id=1, replica_groups=mesh['rep'=2,'blk'=16] {'blk'}, dimensions={0}, use_global_device_ids=true | all-gather | bytes 34816 | tf_op jit(solution)/shard_map/all_gather | solution.py:21
  91.4 18.5 %all_gather.14 = f32[16,16,32]{2,1,0:T(8,128)S(1)} all-gather(f32[1,16,32]{2,1,0:T(8,128)S(1)} %copy.42), channel_id=1, replica_groups=mesh['rep'=2,'blk'=16] {'blk'}, dimensions={0}, use_global_device_ids=true | all-gather | bytes 34816 | tf_op jit(solution)/shard_map/all_gather | solution.py:21
  109.9 10.7 %all-gather.2.cloned.1.call-done = f32[16,16,32,128]{3,2,1,0:T(8,128)} async-done(((f32[1,16,32,128]{3,2,1,0:T(8,128)}), f32[16,16,32,128]{3,2,1,0:T(8,128)}) %all-gather.2.cloned.1.call-update) | async-done | bytes 4194320 | tf_op jit(solution)/shard_map/all_gather | solution.py:21
  120.5 1.0 slice_bitcast_fusion
  121.5 4.6 %slice.54 = f32[15,16,32,128]{3,2,1,0:T(8,128)} slice(f32[16,16,32,128]{3,2,1,0:T(8,128)} %all-gather.2.cloned.1.call-done), slice={[1:16], [0:16], [0:32], [0:128]} | slice | bytes 7864320 | tf_op jit(solution)/shard_map/slice | solution.py:23
  126.1 18.9 %while.14 = (s32[]{:T(128)}, f32[16,32,128]{2,1,0:T(8,128)S(1)}, f32[16,32]{1,0:T(8,128)S(1)}, f32[16,32]{1,0:T(8,128)S(1)}, f32[15,16,32]{2,1,0:T(8,128)S(1)}, ...) while((s32[]{:T(128)}, f32[16,32,128]{2,1,0:T(8,128)S(1)}, f32[16,32]{1,0:T(8,128)S(1)}, ...), condition=%wide.region_5.6_spmd, body=%wide.region_4.5_spmd.sunk | while | flops 199682 | bytes 807013 | solution.py:24
  126.1 1.2 fusion.53
  127.4 1.2 fusion.53
  128.6 1.2 fusion.53
  129.9 1.2 fusion.53
  131.1 1.2 fusion.53
  132.4 1.2 fusion.53
  133.7 1.2 fusion.53
  134.9 1.2 fusion.53
  136.2 1.2 fusion.53
  137.4 1.2 fusion.53
  138.7 1.2 fusion.53
  139.9 1.2 fusion.53
  141.2 1.2 fusion.53
  142.5 1.2 fusion.53
  143.7 1.2 fusion.53
  144.9 0.1 divide_convert_fusion
  145.1 0.4 fusion.17
  145.5 19.5 %all_gather.15 = bf16[16,4096]{1,0:T(8,128)(2,1)S(1)} all-gather(bf16[16,256]{1,0:T(8,128)(2,1)S(1)} %fusion.17), channel_id=1, replica_groups=mesh['rep'=2,'blk'=16] {'blk'}, dimensions={1}, use_global_device_ids=true | all-gather | bytes 139264 | tf_op jit(solution)/shard_map/all_gather | solution.py:109
  165.0 0.1 fusion.21
  165.2 0.2 fusion.41
  165.5 6.3 %fusion.5 = f32[16,1792]{1,0:T(8,128)S(1)} fusion(bf16[2,4096,1792]{2,1,0:T(8,128)(2,1)} %param.26, bf16[16,4096]{1,0:T(8,128)(2,1)S(1)} %all_gather.15, f32[4096]{0:T(1024)S(1)} %convert_element_type.47, f32[16]{0:T(128)S(1)} %add_rsqrt_fusion), kind=kOutput, calls=%fused_computation.12 | convolution fusion | flops 235143168 | bytes 14942272 | tf_op jit(solution)/shard_map/dot_general | solution.py:119
  171.8 0.1 multiply_reduce_fusion
  171.9 12.5 %convolution_multiply_fusion = f32[16,4096]{1,0:T(8,128)} fusion(bf16[1792,4096]{1,0:T(8,128)(2,1)} %param.27, bf16[2,4096,1792]{2,1,0:T(8,128)(2,1)} %param.26, f32[16]{0:T(128)S(1)} %multiply_reduce_fusion, f32[16,1792]{1,0:T(8,128)S(1)} %fusion.5, bf16[16,4096]{1,0:T(8,128)(2,1)S(1)} %all_gather.15, f32[4096]{0:T(1024)S(1)} %convert_element_type.47, ...), kind=kOutput, calls=%fused_computation.16 | convolution fusion | flops 470261760 | bytes 29884544 | tf_op jit(solution)/shard_map/dot_general | solution.py:122
  184.4 0.0 reduce-scatter.2.cloned.1.call-update
  184.5 53.1 %reduce-scatter.2.cloned.1.call-done = f32[16,256]{1,0:T(8,128)} async-done(((f32[16,4096]{1,0:T(8,128)}), f32[16,256]{1,0:T(8,128)}) %reduce-scatter.2.cloned.1.call-update) | async-done | bytes 16400 | tf_op jit(solution)/shard_map/reduce_scatter | solution.py:123
  237.5 1.3 add_convert_fusion
  (43 shorter events, 0.4 us)
Async XLA Ops:
  6.5 138.6 %copy-start = (bf16[4096,256]{1,0:T(8,128)(2,1)S(1)}, bf16[4096,256]{1,0:T(8,128)(2,1)}, u32[]{:S(2)}) copy-start(bf16[4096,256]{1,0:T(8,128)(2,1)} %param.22) | copy-start | bytes 6291460
  6.5 8.6 %copy-start.4 = (bf16[16,4096]{1,0:T(8,128)(2,1)S(1)}, bf16[16,4096]{1,0:T(8,128)(2,1)}, u32[]{:S(2)}) copy-start(bf16[16,4096]{1,0:T(8,128)(2,1)} %param.16) | copy-start | bytes 393220
  6.5 8.7 %copy-start.2 = (s32[16]{0:T(128)S(1)}, s32[16]{0:T(128)}, u32[]{:S(2)}) copy-start(s32[16]{0:T(128)} %param.18) | copy-start | bytes 196
  6.5 3.4 %copy-start.3 = (bf16[2,8,32,1024]{3,2,1,0:T(8,128)(2,1)S(1)}, bf16[2,8,32,1024]{3,2,1,0:T(8,128)(2,1)}, u32[]{:S(2)}) copy-start(bf16[2,8,32,1024]{3,2,1,0:T(8,128)(2,1)} %param.19) | copy-start | bytes 3145732
  6.5 8.7 %copy-start.10 = (s32[8]{0:T(128)S(1)}, s32[8]{0:T(128)}, u32[]{:S(2)}) copy-start(s32[8]{0:T(128)} %param.20) | copy-start | bytes 100
  6.5 8.7 %copy-start.8 = (s32[8]{0:T(128)S(1)}, s32[8]{0:T(128)}, u32[]{:S(2)}) copy-start(s32[8]{0:T(128)} %param.21) | copy-start | bytes 100
  6.6 114.0 %all-gather.2.cloned.1.call-start = ((), (), s32[]{:S(2)}) async-start(), calls=%async_computation.1 | async-start | bytes 4456448 | tf_op jit(solution)/shard_map/all_gather | solution.py:21
  11.1 39.5 %collective-permute-start.1 = (bf16[2,8,32,512]{3,2,1,0:T(8,128)(2,1)}, bf16[2,8,32,512]{3,2,1,0:T(8,128)(2,1)S(1)}, u32[]{:S(2)}, u32[]{:S(2)}) collective-permute-start(bf16[2,8,32,512]{3,2,1,0:T(8,128)(2,1)} %get-tuple-element.73), channel_id=1, source_target_pairs={{0,8},{1,9},{2,10},{3,11},{4,12},{5,13},{6,14},{7,15},{8,0},{9,1},... | collective-permute-start | bytes 1572872 | tf_op jit(solution)/shard_map/ppermute | solution.py:17
  15.1 45.8 %collective-permute-start = (bf16[2,8,32,512]{3,2,1,0:T(8,128)(2,1)}, bf16[2,8,32,512]{3,2,1,0:T(8,128)(2,1)S(1)}, u32[]{:S(2)}, u32[]{:S(2)}) collective-permute-start(bf16[2,8,32,512]{3,2,1,0:T(8,128)(2,1)} %get-tuple-element.72), channel_id=1, source_target_pairs={{0,8},{1,9},{2,10},{3,11},{4,12},{5,13},{6,14},{7,15},{8,0},{9,1},... | collective-permute-start | bytes 1572872 | tf_op jit(solution)/shard_map/ppermute | solution.py:17
  65.8 2.6 %copy-start.6 = (bf16[4096]{0:T(1024)(128)(2,1)S(1)}, bf16[4096]{0:T(1024)(128)(2,1)}, u32[]{:S(2)}) copy-start(bf16[4096]{0:T(1024)(128)(2,1)} %param.23) | copy-start | bytes 24580
  68.3 169.3 %reduce-scatter.2.cloned.1.call-start = ((), (), s32[]{:S(2)}) async-start(), calls=%async_computation.2 | async-start | bytes 278528 | tf_op jit(solution)/shard_map/reduce_scatter | solution.py:123
  126.1 19.0 %copy-start.5 = (bf16[16,256]{1,0:T(8,128)(2,1)S(1)}, bf16[16,256]{1,0:T(8,128)(2,1)}, u32[]{:S(2)}) copy-start(bf16[16,256]{1,0:T(8,128)(2,1)} %param.15) | copy-start | bytes 24580
  126.1 39.1 %copy-start.9 = (bf16[4096,4]{0,1:T(4,128)(2,1)S(1)}, bf16[4096,4]{0,1:T(4,128)(2,1)}, u32[]{:S(2)}) copy-start(bf16[4096,4]{0,1:T(4,128)(2,1)} %param.24) | copy-start | bytes 98308
  126.1 39.3 %copy-start.7 = (s32[16,2]{0,1:T(2,128)S(1)}, s32[16,2]{0,1:T(2,128)}, u32[]{:S(2)}) copy-start(s32[16,2]{0,1:T(2,128)} %param.25) | copy-start | bytes 388
  171.9 67.0 %copy-start.1 = (bf16[4096,256]{1,0:T(8,128)(2,1)S(1)}, bf16[4096,256]{1,0:T(8,128)(2,1)}, u32[]{:S(2)}) copy-start(bf16[4096,256]{1,0:T(8,128)(2,1)} %param.22) | copy-start | bytes 6291460
Sparse Core Ops, SparseCore 0:
  68.4 52.1 all-gather.1
  184.6 52.9 reduce-scatter.1
where the time goes:
time: 246 us
  waiting for transfers between devices  109 us (44%)
  blocking collectives  60.2 us (24%)
  matrix products  21.3 us (9%)
  other arithmetic  20.9 us (8%)
  local copies, waits for them, and re-layouts  16.4 us (7%)
  between operations  13.7 us (6%)
  starting transfers between devices  4.17 us (2%)
    reduce_scatter x1, waiting for transfers between devices, on_device(): moe = lax.psum_scatter(term, 'blk', scatter_dimension=1, tiled=True)  53.1 us
    ppermute x2, waiting for transfers between devices, shifted(): lax.ppermute(shard, axis, [(i, (i + by) % count) for i in range(count)])  45 us
    all_gather x2, blocking collectives, merged(): pieces = jax.tree.map(lambda part: lax.all_gather(part, axis), value)  40.6 us
    all_gather x1, blocking collectives, on_device(): mixed = lax.all_gather(local_mixed, 'blk', axis=1, tiled=True)  19.5 us
    add x15, other arithmetic, merge_pair(): early_out * early_scale[..., None] + late_out * late_scale[..., None]  18.2 us
    dot_general x1, matrix products, on_device(): jnp.dot(act, down_proj, preferred_element_type=jnp.float32)  12.5 us
    all_gather x1, waiting for transfers between devices, merged(): pieces = jax.tree.map(lambda part: lax.all_gather(part, axis), value)  10.7 us
    dot_general x1, matrix products, on_device(): jnp.dot(normed, gate_up[0], preferred_element_type=jnp.float32)  6.29 us
  transfers between devices with their start and end apart: 4, of which 4 were waited for; matrix products, arithmetic and copies ran while one was open for 1% of the time, Pallas kernels for 0%

commit v1 on v0

--- a/solution.py
+++ b/solution.py
@@ -1,8 +1,11 @@
+import functools
 import math
 
 import jax
 import jax.numpy as jnp
 from jax import lax
+from jax.experimental import pallas as pl
+from jax.experimental.pallas import tpu as pltpu
 from jax.sharding import PartitionSpec as P
 
 QUERY_HEADS = 32
@@ -10,11 +13,6 @@
 HEAD_SIZE = 128
 EXPERTS = 4
 FF = 7168
-
-
-def shifted(shard, axis, by):
-    count = lax.axis_size(axis)
-    return lax.ppermute(shard, axis, [(i, (i + by) % count) for i in range(count)])
 
 
 def merged(value, axis, join):
@@ -68,7 +66,7 @@
     return jnp.sum(gates[:, :, None] * chosen, axis=1)
 
 
-def on_device(
+def plain_layer(
     hidden,
     queries,
     cache_kv,
@@ -85,16 +83,15 @@
 ):
     cycle_size = lax.axis_size("blk")
     dev_index = lax.axis_index("blk")
-    half_cycle = cycle_size // 2
     ctx_rows = cache_kv.shape[2]
-    column_half = inserted_key_value.shape[3] // 2
-    first_cols = shifted(inserted_key_value[..., :column_half], "blk", half_cycle)
-    second_cols = shifted(inserted_key_value[..., column_half:], "blk", -half_cycle)
-    arrived = jnp.concatenate([first_cols, second_cols], axis=3)
-    cache = cache_kv.at[:, insert_slot].set(arrived)
+    half = cycle_size * ctx_rows // 2
+    cache = cache_kv.at[:, insert_slot].set(inserted_key_value)
     slot_lengths = cache_len.at[insert_slot].set(prefix_len)
     positions = dev_index * ctx_rows + jnp.arange(ctx_rows, dtype=jnp.int32)
-    valid = positions[None, :] < slot_lengths[:, None]
+    rolled = jnp.where(positions < half, positions + half, positions - half)
+    inserted = jnp.zeros(cache_len.shape, jnp.bool_).at[insert_slot].set(True)
+    held = jnp.where(inserted[:, None], rolled[None, :], positions[None, :])
+    valid = held < slot_lengths[:, None]
     partial_value, peak, totals = block_attention(queries, cache[0], cache[1], valid)
     slot_list = queries.shape[0]
     summed, highest, all_totals = merged((partial_value, peak, totals), "blk", merge_pair)
@@ -124,6 +121,383 @@
     return (local_mixed.astype(jnp.float32) + moe).astype(jnp.bfloat16)
 
 
+NEG = -1e30
+GU_CHUNKS = 8
+MESH = pl.DeviceIdType.MESH
+
+
+def fused_kernel(
+    n,
+    cache_len,
+    insert_slot,
+    prefix_len,
+    expert_ids,
+    hidden_h,
+    queries_h,
+    cache_h,
+    inserted_h,
+    out_w_h,
+    gain_h,
+    router_h,
+    gate_up_h,
+    down_h,
+    out_ref,
+    hidden,
+    queries,
+    kv,
+    out_w,
+    gain,
+    router,
+    gate_up,
+    down,
+    part_send,
+    part_recv,
+    attn_all,
+    mixed_all,
+    normed_ref,
+    gate_acc,
+    up_acc,
+    term_send,
+    term_recv,
+    in_sem,
+    gu_sem,
+    down_sem,
+    send_sem,
+    recv_sem,
+):
+    me = lax.axis_index("blk")
+    slots = queries.shape[0]
+    group = QUERY_HEADS // KEY_VALUE_HEADS
+    inserts = insert_slot.shape[0]
+    ctx = kv.shape[2]
+    width = out_w.shape[1]
+    depth = gate_up.shape[1] // GU_CHUNKS
+    units = gate_up.shape[2]
+
+    copies = [
+        pltpu.make_async_copy(s, d, in_sem.at[i])
+        for i, (s, d) in enumerate(
+            [
+                (queries_h, queries),
+                (cache_h, kv.at[:, pl.ds(0, slots)]),
+                (inserted_h, kv.at[:, pl.ds(slots, inserts)]),
+                (hidden_h, hidden),
+                (gain_h, gain),
+                (router_h, router),
+                (out_w_h, out_w),
+            ]
+        )
+    ]
+    for copy in copies:
+        copy.start()
+
+    def gu_copy(k):
+        rows = pl.ds(pl.multiple_of(k * depth, depth), depth)
+        return pltpu.make_async_copy(gate_up_h.at[:, rows], gate_up.at[:, rows], gu_sem.at[k])
+
+    def columns(c):
+        return pl.ds(pl.multiple_of(c * width, width), width)
+
+    def down_copy(c):
+        return pltpu.make_async_copy(
+            down_h.at[:, columns(c)], down.at[:, columns(c)], down_sem.at[c]
+        )
+
+    def each(count, step):
+        lax.fori_loop(0, count, lambda i, carry: (step(i), carry)[1], 0)
+
+    def peer_of(i):
+        return lax.rem(me + 1 + i, n)
+
+    barrier = pltpu.get_barrier_semaphore()
+    each(
+        n - 1,
+        lambda i: pl.semaphore_signal(
+            barrier, inc=1, device_id={"blk": peer_of(i)}, device_id_type=MESH
+        ),
+    )
+    each(GU_CHUNKS, lambda k: gu_copy(k).start())
+    each(n, lambda i: down_copy(peer_of(i)).start())
+
+    entries = slots + inserts
+    cols = entries * ctx
+    col = lax.broadcasted_iota(jnp.int32, (1, cols), 1)
+    shift = ctx.bit_length() - 1
+    entry = lax.shift_right_logical(col, jnp.full_like(col, shift))
+    row_at = me * ctx + (col & (ctx - 1))
+    half = n * ctx // 2
+    rolled = jnp.where(row_at < half, row_at + half, row_at - half)
+    position = jnp.where(entry < slots, row_at, rolled)
+    slot_of = entry
+    length = jnp.zeros_like(col)
+    for s in range(slots):
+        length = jnp.where(entry == s, cache_len[s], length)
+    for j in range(inserts):
+        slot_of = jnp.where(entry == insert_slot[j], -1, slot_of)
+    for j in range(inserts):
+        slot_of = jnp.where(entry == slots + j, insert_slot[j], slot_of)
+        length = jnp.where(entry == slots + j, prefix_len[j], length)
+    slot_of = jnp.where(position < length, slot_of, -1)
+    rows = group * slots
+    row_slot = lax.broadcasted_iota(jnp.int32, (rows, 1), 0) & (slots - 1)
+    mask = row_slot == slot_of
+    lane = lax.broadcasted_iota(jnp.int32, (rows, HEAD_SIZE), 1)
+    place = lane & (HEAD_SIZE // 2 - 1)
+    low_lane = lane[:slots] < HEAD_SIZE // 2
+
+    for copy in copies[:3]:
+        copy.wait()
+    per_group = group // 2
+    for g in range(KEY_VALUE_HEADS):
+        q = jnp.concatenate(
+            [
+                queries[:, (g * group + r) * HEAD_SIZE : (g * group + r + 1) * HEAD_SIZE]
+                for r in range(group)
+            ],
+            axis=0,
+        )
+        span = slice(g * HEAD_SIZE, (g + 1) * HEAD_SIZE)
+        keys = kv[0, :, :, span].reshape(cols, HEAD_SIZE)
+        values = kv[1, :, :, span].reshape(cols, HEAD_SIZE)
+        scores = lax.dot_general(
+            q, keys, (((1,), (1,)), ((), ())), preferred_element_type=jnp.float32
+        ) * (1.0 / math.sqrt(HEAD_SIZE))
+        peak = jnp.max(jnp.where(mask, scores, NEG), axis=-1, keepdims=True)
+        peak = peak.astype(jnp.bfloat16).astype(jnp.float32)
+        weights = jnp.where(mask, jnp.exp(scores - peak), 0.0).astype(jnp.bfloat16)
+        total = jnp.sum(weights.astype(jnp.float32), axis=-1, keepdims=True)
+        summed = jnp.dot(weights, values, preferred_element_type=jnp.float32)
+        total_high = total.astype(jnp.bfloat16).astype(jnp.float32)
+        stats = jnp.where(
+            place == 0, peak, jnp.where(place == 1, total_high, total - total_high)
+        )
+        for h in range(per_group):
+            at = 2 * h * slots
+            c = g * per_group + h
+            part_send[c, 0 : 2 * slots, :] = summed[at : at + 2 * slots].astype(jnp.bfloat16)
+            part_send[c, 2 * slots : 3 * slots, :] = jnp.where(
+                low_lane, stats[at : at + slots], stats[at + slots : at + 2 * slots]
+            ).astype(jnp.bfloat16)
+    part_recv[me] = part_send[me]
+
+    pl.semaphore_wait(barrier, n - 1)
+
+    def part_copy(to, slot):
+        return pltpu.make_async_remote_copy(
+            src_ref=part_send.at[to],
+            dst_ref=part_recv.at[slot],
+            send_sem=send_sem.at[0, to],
+            recv_sem=recv_sem.at[0, slot],
+            device_id={"blk": to},
+            device_id_type=MESH,
+        )
+
+    def share_copy(ref, phase, to, slot):
+        return pltpu.make_async_remote_copy(
+            src_ref=ref.at[:, columns(slot)],
+            dst_ref=ref.at[:, columns(slot)],
+            send_sem=send_sem.at[phase, to],
+            recv_sem=recv_sem.at[phase, slot],
+            device_id={"blk": to},
+            device_id_type=MESH,
+        )
+
+    def term_copy(to, slot):
+        return pltpu.make_async_remote_copy(
+            src_ref=term_send.at[to],
+            dst_ref=term_recv.at[slot],
+            send_sem=send_sem.at[3, to],
+            recv_sem=recv_sem.at[3, slot],
+            device_id={"blk": to},
+            device_id_type=MESH,
+        )
+
+    each(n - 1, lambda i: part_copy(peer_of(i), me).start())
+    each(n - 1, lambda i: part_copy(peer_of(i), peer_of(i)).wait_recv())
+
+    stat_parts = [part_recv[i, 2 * slots : 3 * slots, :].astype(jnp.float32) for i in range(n)]
+    highest = functools.reduce(jnp.maximum, stat_parts)
+    sums = [jnp.zeros((slots, HEAD_SIZE), jnp.float32) for _ in range(2)]
+    totals = [jnp.zeros((slots, 1), jnp.float32) for _ in range(2)]
+    for i in range(n):
+        scale = jnp.exp(stat_parts[i] - highest)
+        for h in range(2):
+            at = h * (HEAD_SIZE // 2)
+            weight = scale[:, at : at + 1]
+            totals[h] += weight * (
+                stat_parts[i][:, at + 1 : at + 2] + stat_parts[i][:, at + 2 : at + 3]
+            )
+            sums[h] += weight * part_recv[i, h * slots : (h + 1) * slots, :].astype(jnp.float32)
+    attn = jnp.concatenate([sums[h] / totals[h] for h in range(2)], axis=1)
+    attn_all[:, columns(me)] = attn.astype(jnp.bfloat16)
+    each(n - 1, lambda i: share_copy(attn_all, 1, peer_of(i), me).start())
+    for copy in copies[3:]:
+        copy.wait()
+    each(n - 1, lambda i: share_copy(attn_all, 1, peer_of(i), peer_of(i)).wait_recv())
+
+    local_mixed = (
+        hidden[...].astype(jnp.float32)
+        + jnp.dot(attn_all[...], out_w[...], preferred_element_type=jnp.float32)
+    ).astype(jnp.bfloat16)
+    mixed_all[:, columns(me)] = local_mixed
+    each(n - 1, lambda i: share_copy(mixed_all, 2, peer_of(i), me).start())
+    each(n - 1, lambda i: share_copy(mixed_all, 2, peer_of(i), peer_of(i)).wait_recv())
+
+    mixed = mixed_all[...].astype(jnp.float32)
+    scale = lax.rsqrt(jnp.mean(mixed * mixed, axis=-1, keepdims=True) + 1e-05)
+    normed = (mixed * scale * gain[...].astype(jnp.float32)).astype(jnp.bfloat16)
+    normed_ref[...] = normed
+    normed = normed.astype(jnp.float32)
+    router_rows = router[...].astype(jnp.float32)
+    logits = [
+        jnp.sum(normed * router_rows[e : e + 1], axis=-1, keepdims=True) for e in range(EXPERTS)
+    ]
+    row = lax.broadcasted_iota(jnp.int32, (slots, 1), 0)
+    chosen = []
+    for k in range(2):
+        ids = jnp.zeros_like(row)
+        for s in range(slots):
+            ids = jnp.where(row == s, expert_ids[2 * s + k], ids)
+        chosen.append(ids)
+    picked = [
+        sum(jnp.where(chosen[k] == e, logits[e], 0.0) for e in range(EXPERTS)) for k in range(2)
+    ]
+    expert_now = (me * units) // FF
+    share = jnp.where(chosen[0] == expert_now, jax.nn.sigmoid(picked[0] - picked[1]), 0.0)
+    share += jnp.where(chosen[1] == expert_now, jax.nn.sigmoid(picked[1] - picked[0]), 0.0)
+
+    gate_acc[...] = jnp.zeros_like(gate_acc)
+    up_acc[...] = jnp.zeros_like(up_acc)
+
+    def gu_step(k):
+        gu_copy(k).wait()
+        rows = pl.ds(pl.multiple_of(k * depth, depth), depth)
+        piece = normed_ref[:, rows]
+        gate_acc[...] += jnp.dot(piece, gate_up[0, rows, :], preferred_element_type=jnp.float32)
+        up_acc[...] += jnp.dot(piece, gate_up[1, rows, :], preferred_element_type=jnp.float32)
+
+    each(GU_CHUNKS, gu_step)
+    gate = gate_acc[...]
+    act = (gate * jax.nn.sigmoid(gate) * up_acc[...]).astype(jnp.bfloat16)
+
+    def term_of(c):
+        down_copy(c).wait()
+        return share * jnp.dot(act, down[:, columns(c)], preferred_element_type=jnp.float32)
+
+    def term_step(i):
+        c = peer_of(i)
+        term_send[c] = term_of(c).astype(jnp.bfloat16)
+        term_copy(c, me).start()
+
+    each(n - 1, term_step)
+    total = local_mixed.astype(jnp.float32) + term_of(me)
+    term_recv[me] = jnp.zeros((slots, width), jnp.bfloat16)
+    each(n - 1, lambda i: term_copy(peer_of(i), peer_of(i)).wait_recv())
+    for i in range(n):
+        total += term_recv[i].astype(jnp.float32)
+    out_ref[...] = total.astype(jnp.bfloat16)
+
+    def drain(i):
+        c = peer_of(i)
+        part_copy(c, me).wait_send()
+        share_copy(attn_all, 1, c, me).wait_send()
+        share_copy(mixed_all, 2, c, me).wait_send()
+        term_copy(c, me).wait_send()
+
+    each(n - 1, drain)
+
+
+def fused_layer(
+    n,
+    hidden,
+    queries,
+    cache_kv,
+    cache_len,
+    inserted_key_value,
+    insert_slot,
+    prefix_len,
+    out_weight,
+    norm_gain,
+    router_weight,
+    expert_ids,
+    gate_up,
+    down_proj,
+):
+    slots, features = queries.shape
+    entries = slots + insert_slot.shape[0]
+    width = out_weight.shape[1]
+    units = gate_up.shape[2]
+    any_space = pl.BlockSpec(memory_space=pl.ANY)
+    smem = pl.BlockSpec(memory_space=pltpu.SMEM)
+    bf16, f32 = jnp.bfloat16, jnp.float32
+    return pl.pallas_call(
+        functools.partial(fused_kernel, n),
+        out_shape=jax.ShapeDtypeStruct((slots, width), bf16),
+        in_specs=[smem] * 4 + [any_space] * 9,
+        out_specs=pl.BlockSpec(memory_space=pltpu.VMEM),
+        scratch_shapes=[
+            pltpu.VMEM((slots, width), bf16),
+            pltpu.VMEM((slots, features), bf16),
+            pltpu.VMEM((2, entries) + cache_kv.shape[2:], bf16),
+            pltpu.VMEM(out_weight.shape, bf16),
+            pltpu.VMEM((1, features), bf16),
+            pltpu.VMEM((EXPERTS, features), bf16),
+            pltpu.VMEM(gate_up.shape, bf16),
+            pltpu.VMEM(down_proj.shape, bf16),
+            pltpu.VMEM((n, 3 * slots, HEAD_SIZE), bf16),
+            pltpu.VMEM((n, 3 * slots, HEAD_SIZE), bf16),
+            pltpu.VMEM((slots, features), bf16),
+            pltpu.VMEM((slots, features), bf16),
+            pltpu.VMEM((slots, features), bf16),
+            pltpu.VMEM((slots, units), f32),
+            pltpu.VMEM((slots, units), f32),
+            pltpu.VMEM((n, slots, width), bf16),
+            pltpu.VMEM((n, slots, width), bf16),
+            pltpu.SemaphoreType.DMA((7,)),
+            pltpu.SemaphoreType.DMA((GU_CHUNKS,)),
+            pltpu.SemaphoreType.DMA((n,)),
+            pltpu.SemaphoreType.DMA((4, n)),
+            pltpu.SemaphoreType.DMA((4, n)),
+        ],
+        compiler_params=pltpu.CompilerParams(
+            collective_id=0, has_side_effects=True, vmem_limit_bytes=60 * 1024 * 1024
+        ),
+        name="layer",
+    )(
+        cache_len,
+        insert_slot,
+        prefix_len,
+        expert_ids.reshape(-1),
+        hidden,
+        queries,
+        cache_kv,
+        inserted_key_value,
+        out_weight,
+        norm_gain.reshape(1, features),
+        router_weight.T,
+        gate_up,
+        down_proj,
+    )
+
+
+def on_device(*args):
+    n = lax.axis_size("blk")
+    queries, cache_kv, out_weight, gate_up = args[1], args[2], args[7], args[11]
+    ctx, slots = cache_kv.shape[2], queries.shape[0]
+    fits = (
+        QUERY_HEADS == 2 * n
+        and out_weight.shape[1] == 2 * HEAD_SIZE
+        and ctx % 16 == 0
+        and ctx & (ctx - 1) == 0
+        and slots % 16 == 0
+        and slots & (slots - 1) == 0
+        and gate_up.shape[1] % (128 * GU_CHUNKS) == 0
+        and gate_up.shape[2] % 128 == 0
+        and FF % gate_up.shape[2] == 0
+    )
+    return fused_layer(n, *args) if fits else plain_layer(*args)
+
+
 def solution(mesh):
     in_specs = (
         P("rep", "blk"),

time: 246 us -> 43.1 us (0.18)
  waiting for transfers between devices: 109 us -> 0 us
  blocking collectives: 60.2 us -> 0 us
  Pallas kernels: 0 us -> 38.9 us
  matrix products: 21.3 us -> 0 us
  other arithmetic: 20.9 us -> 0 us
  between operations: 13.7 us -> 0.01 us
  local copies, waits for them, and re-layouts: 16.4 us -> 3.95 us
  starting transfers between devices: 4.17 us -> 0 us
    all_gather x3 -> x0, blocking collectives: 60.2 us -> none  [the longest x2 40.6 us: merged(): pieces = jax.tree.map(lambda part: lax.all_gather(part, axis), value)]
    reduce_scatter x1 -> x0, waiting for transfers between devices: 53.1 us -> none  [on_device(): moe = lax.psum_scatter(term, 'blk', scatter_dimension=1, tiled=True)]
    ppermute x2 -> x0, waiting for transfers between devices: 45 us -> none  [shifted(): lax.ppermute(shard, axis, [(i, (i + by) % count) for i in range(count)])]
    pallas_call x0 -> x1, Pallas kernels: none -> 38.9 us  [fused_layer(): pl.pallas_call(functools.partial(fused_kernel, n), out_shape=jax.ShapeDty...]
    dot_general x6 -> x0, matrix products: 21.3 us -> none  [the longest x1 12.5 us: on_device(): jnp.dot(act, down_proj, preferred_element_type=jnp.float32)]
    add x31 -> x0, other arithmetic: 18.5 us -> none  [the longest x15 18.2 us: merge_pair(): early_out * early_scale[..., None] + late_out * late_scale[..., None]]
    all_gather x1 -> x0, waiting for transfers between devices: 10.7 us -> none  [merged(): pieces = jax.tree.map(lambda part: lax.all_gather(part, axis), value)]
    slice x5 -> x0, local copies, waits for them, and re-layouts: 7.38 us -> none  [the longest x3 4.57 us: merged(): tail = jax.tree.map(lambda part: part[1:], pieces)]
  transfers between devices with their start and end apart: 4 -> 0, of which waited for: 4 -> 0; matrix products, arithmetic and copies ran while one was open for 1% -> 0% of each run, Pallas kernels for 0% -> 0%
where the time goes in v1:
time: 43.1 us; the launch traced here: 42.8 us
  Pallas kernels  38.9 us (90%)
  local copies, waits for them, and re-layouts  3.95 us (9%)
    pallas_call x1, Pallas kernels, fused_layer(): pl.pallas_call(functools.partial(fused_kernel, n), out_shape=jax.ShapeDty...  38.9 us
    unnamed x2, local copies, waits for them, and re-layouts  2.05 us
    reshape x1, local copies, waits for them, and re-layouts, fused_layer(): norm_gain.reshape(1, features)  1.3 us

profile of v1, /device:TPU:0, one launch (start us, length us, event | category | flops | bytes accessed | tf_op | source)
XLA Modules:
  0.0 42.8 jit_solution(10337646047637395940)
XLA Ops:
  0.0 0.8 %copy.15 = s32[16,2]{1,0:T(8,128)S(1)} copy(s32[16,2]{0,1:T(2,128)} %param.23) | data formatting | bytes 256 | tf_op args[10]
  0.8 0.6 %reshape.6.expert_ids = s32[32]{0:T(128)} reshape(s32[16,2]{1,0:T(8,128)S(1)} %copy.15) | data formatting | bytes 256 | tf_op jit(solution)/shard_map/reshape | solution.py:470
  1.4 1.3 %reshape.7.gain_h = bf16[1,4096]{1,0:T(2,128)(2,1)} reshape(bf16[4096]{0:T(1024)(128)(2,1)} %param.21) | data formatting | bytes 16384 | tf_op jit(solution)/shard_map/reshape | solution.py:476
  2.7 38.9 %layer.1 = bf16[16,256]{1,0:T(8,128)(2,1)} custom-call(s32[16]{0:T(128)} %cache_len.1, s32[8]{0:T(128)} %insert_slot.1, s32[8]{0:T(128)} %prefix_len.1, s32[32]{0:T(128)} %reshape.6.expert_ids, bf16[16,256]{1,0:T(8,128)(2,1)} %hidden_h.1, bf16[16,4096]{1,0:T(8,128)(2,1)} %queries_h.1, bf16[2,16,32,1024]{3,2,1,0:T(8,128)(2,1)} %cache_h.1, ...), custom_call_target="tpu_custom_call" | custom-call | tf_op jit(solution)/shard_map/layer/pallas_call | solution.py:433
  41.5 1.3 %copy.17 = bf16[16,256]{1,0:T(8,128)(2,1)} copy(bf16[16,256]{1,0:T(8,128)(2,1)} %layer.1) | data formatting | bytes 16384

commit v2 on v1

--- a/solution.py
+++ b/solution.py
@@ -203,14 +203,19 @@
             down_h.at[:, columns(c)], down.at[:, columns(c)], down_sem.at[c]
         )
 
+    def every(count, step):
+        for i in range(count):
+            step(i)
+
     def each(count, step):
         lax.fori_loop(0, count, lambda i, carry: (step(i), carry)[1], 0)
 
     def peer_of(i):
-        return lax.rem(me + 1 + i, n)
+        later = me + 1 + i
+        return jnp.where(later >= n, later - n, later)
 
     barrier = pltpu.get_barrier_semaphore()
-    each(
+    every(
         n - 1,
         lambda i: pl.semaphore_signal(
             barrier, inc=1, device_id={"blk": peer_of(i)}, device_id_type=MESH
@@ -312,8 +317,8 @@
             device_id_type=MESH,
         )
 
-    each(n - 1, lambda i: part_copy(peer_of(i), me).start())
-    each(n - 1, lambda i: part_copy(peer_of(i), peer_of(i)).wait_recv())
+    every(n - 1, lambda i: part_copy(peer_of(i), me).start())
+    every(n - 1, lambda i: part_copy(peer_of(i), peer_of(i)).wait_recv())
 
     stat_parts = [part_recv[i, 2 * slots : 3 * slots, :].astype(jnp.float32) for i in range(n)]
     highest = functools.reduce(jnp.maximum, stat_parts)
@@ -330,22 +335,24 @@
             sums[h] += weight * part_recv[i, h * slots : (h + 1) * slots, :].astype(jnp.float32)
     attn = jnp.concatenate([sums[h] / totals[h] for h in range(2)], axis=1)
     attn_all[:, columns(me)] = attn.astype(jnp.bfloat16)
-    each(n - 1, lambda i: share_copy(attn_all, 1, peer_of(i), me).start())
+    every(n - 1, lambda i: share_copy(attn_all, 1, peer_of(i), me).start())
     for copy in copies[3:]:
         copy.wait()
-    each(n - 1, lambda i: share_copy(attn_all, 1, peer_of(i), peer_of(i)).wait_recv())
+    every(n - 1, lambda i: share_copy(attn_all, 1, peer_of(i), peer_of(i)).wait_recv())
 
     local_mixed = (
         hidden[...].astype(jnp.float32)
         + jnp.dot(attn_all[...], out_w[...], preferred_element_type=jnp.float32)
     ).astype(jnp.bfloat16)
     mixed_all[:, columns(me)] = local_mixed
-    each(n - 1, lambda i: share_copy(mixed_all, 2, peer_of(i), me).start())
-    each(n - 1, lambda i: share_copy(mixed_all, 2, peer_of(i), peer_of(i)).wait_recv())
+    every(n - 1, lambda i: share_copy(mixed_all, 2, peer_of(i), me).start())
+    every(n - 1, lambda i: share_copy(mixed_all, 2, peer_of(i), peer_of(i)).wait_recv())
 
     mixed = mixed_all[...].astype(jnp.float32)
     scale = lax.rsqrt(jnp.mean(mixed * mixed, axis=-1, keepdims=True) + 1e-05)
-    normed = (mixed * scale * gain[...].astype(jnp.float32)).astype(jnp.bfloat16)
+    gains = gain[...].astype(jnp.float32)
+    gain_row = jnp.concatenate([gains[i : i + 1] for i in range(gains.shape[0])], axis=1)
+    normed = (mixed * scale * gain_row).astype(jnp.bfloat16)
     normed_ref[...] = normed
     normed = normed.astype(jnp.float32)
     router_rows = router[...].astype(jnp.float32)
@@ -357,7 +364,7 @@
     for k in range(2):
         ids = jnp.zeros_like(row)
         for s in range(slots):
-            ids = jnp.where(row == s, expert_ids[2 * s + k], ids)
+            ids = jnp.where(row == s, expert_ids[k, s], ids)
         chosen.append(ids)
     picked = [
         sum(jnp.where(chosen[k] == e, logits[e], 0.0) for e in range(EXPERTS)) for k in range(2)
@@ -392,7 +399,7 @@
     each(n - 1, term_step)
     total = local_mixed.astype(jnp.float32) + term_of(me)
     term_recv[me] = jnp.zeros((slots, width), jnp.bfloat16)
-    each(n - 1, lambda i: term_copy(peer_of(i), peer_of(i)).wait_recv())
+    every(n - 1, lambda i: term_copy(peer_of(i), peer_of(i)).wait_recv())
     for i in range(n):
         total += term_recv[i].astype(jnp.float32)
     out_ref[...] = total.astype(jnp.bfloat16)
@@ -404,7 +411,7 @@
         share_copy(mixed_all, 2, c, me).wait_send()
         term_copy(c, me).wait_send()
 
-    each(n - 1, drain)
+    every(n - 1, drain)
 
 
 def fused_layer(
@@ -440,7 +447,7 @@
             pltpu.VMEM((slots, features), bf16),
             pltpu.VMEM((2, entries) + cache_kv.shape[2:], bf16),
             pltpu.VMEM(out_weight.shape, bf16),
-            pltpu.VMEM((1, features), bf16),
+            pltpu.VMEM((features // HEAD_SIZE, HEAD_SIZE), bf16),
             pltpu.VMEM((EXPERTS, features), bf16),
             pltpu.VMEM(gate_up.shape, bf16),
             pltpu.VMEM(down_proj.shape, bf16),
@@ -467,13 +474,13 @@
         cache_len,
         insert_slot,
         prefix_len,
-        expert_ids.reshape(-1),
+        expert_ids.T,
         hidden,
         queries,
         cache_kv,
         inserted_key_value,
         out_weight,
-        norm_gain.reshape(1, features),
+        norm_gain.reshape(-1, HEAD_SIZE),
         router_weight.T,
         gate_up,
         down_proj,

time: 43.1 us -> 40.2 us (0.933)
  local copies, waits for them, and re-layouts: 3.95 us -> 1.3 us
    reshape x2 -> x0, local copies, waits for them, and re-layouts: 1.9 us -> none  [the longest x1 1.3 us: fused_layer(): norm_gain.reshape(1, features)]
    unnamed x2 -> x1, local copies, waits for them, and re-layouts: 2.05 us -> 1.3 us
where the time goes in v2:
time: 40.2 us; the launch traced here: 40 us
  Pallas kernels  38.7 us (96%)
  local copies, waits for them, and re-layouts  1.3 us (3%)
    pallas_call x1, Pallas kernels, fused_layer(): pl.pallas_call(functools.partial(fused_kernel, n), out_shape=jax.ShapeDty...  38.7 us
    unnamed x1, local copies, waits for them, and re-layouts  1.3 us

profile of v2, /device:TPU:0, one launch (start us, length us, event | category | flops | bytes accessed | tf_op | source)
XLA Modules:
  0.0 40.0 jit_solution(12316434873251199182)
XLA Ops:
  0.0 38.7 %layer.1 = bf16[16,256]{1,0:T(8,128)(2,1)} custom-call(s32[16]{0:T(128)} %cache_len.1, s32[8]{0:T(128)} %insert_slot.1, s32[8]{0:T(128)} %prefix_len.1, s32[2,16]{1,0:T(2,128)} %bitcast.5, bf16[16,256]{1,0:T(8,128)(2,1)} %hidden_h.1, bf16[16,4096]{1,0:T(8,128)(2,1)} %queries_h.1, bf16[2,16,32,1024]{3,2,1,0:T(8,128)(2,1)} %cache_h.1, ...), custom_call_target="tpu_custom_call" | custom-call | tf_op jit(solution)/shard_map/layer/pallas_call | solution.py:440
  38.7 1.3 %copy.15 = bf16[16,256]{1,0:T(8,128)(2,1)} copy(bf16[16,256]{1,0:T(8,128)(2,1)} %layer.1) | data formatting | bytes 16384
